TPU v7x, 32 devices: a whole 2x2x4 slice. The times are simulated.
32 devices in a mesh: dp: 8 (over z, core), seq: 4 (over y, x).
Axes of the slice: x: 2, y: 2, z: 4, core: 2. Of those that a mesh axis runs over, the one named last changes fastest.
Arguments:
- tokens: bfloat16 [32, 256, 1024], P(('dp', 'seq')), may hold values from -6 to 6
- queries: bfloat16 [32, 256, 1024], P(('dp', 'seq')), may hold values from -240 to 240
- keys: bfloat16 [32, 256, 1024], P(('dp', 'seq')), may hold values from -7 to 7
- values: bfloat16 [32, 256, 1024], P(('dp', 'seq')), may hold values from -6 to 6
- ln_gain: bfloat16 [1024], replicated, may hold values from 0.5 to 1.5
- mean_in: bfloat16 [1024, 2048], P(None, 'seq'), may hold values from -0.1875 to 0.1875
- sigma_in: bfloat16 [1024, 2048], P(None, 'seq'), may hold values from 0.0039978027 to 0.029907227
- noise_in: bfloat16 [1024, 2048], P(None, 'seq'), may hold values from -4 to 4
- mean_out: bfloat16 [2048, 1024], P('seq'), may hold values from -0.125 to 0.125
- sigma_out: bfloat16 [2048, 1024], P('seq'), may hold values from 0.0019989014 to 0.014953613
- noise_out: bfloat16 [2048, 1024], P('seq'), may hold values from -4 to 4
- flip_in: int32 [32, 1024], P('dp'), may hold values from -1 to 1, as said below
- flip_mid: int32 [32, 2048], P('dp', 'seq'), may hold values from -1 to 1, as said below
- flip_hidden: int32 [32, 2048], P('dp', 'seq'), may hold values from -1 to 1, as said below
- flip_out: int32 [32, 1024], P('dp'), may hold values from -1 to 1, as said below
- cotangent: bfloat16 [32, 256, 1024], P(('dp', 'seq')), may hold values from -0.75 to 0.75
Outputs:
- block_out: bfloat16 [32, 256, 1024], P(('dp', 'seq'))
- resid_grad: bfloat16 [32, 256, 1024], P(('dp', 'seq'))
- grad_mean_in: float32 [1024, 2048], P(None, 'seq')
- grad_sigma_in: float32 [1024, 2048], P(None, 'seq')
- grad_mean_out: float32 [2048, 1024], P('seq')
- grad_sigma_out: float32 [2048, 1024], P('seq')
Inputs may be any that keep to these rules, and one draw needn't show every extreme that they name: `flip_in`: each entry is -1 or +1. `flip_mid`: each entry is -1 or +1. `flip_hidden`: each entry is -1 or +1. `flip_out`: each entry is -1 or +1.
All inputs are finite; a program needn't handle non-finite values.
Results may differ from a plain program's by a relative error of at most 0.018.
Values may be sent and summed in bfloat16 or wider, within the bound.
A program may use at most 128 MiB of HBM per device.

v0:
```python
import jax
import jax.numpy as jnp
from jax import lax
from jax.sharding import PartitionSpec as P

HEADS = 16


def gelu_slope(pre):
    cdf = 0.5 * (1.0 + lax.erf(pre * 0.7071067811865476))
    pdf = jnp.exp(-0.5 * pre * pre) * 0.3989422804014327
    return cdf + pre * pdf


def contract_first(left, right):
    return lax.dot_general(
        left, right, (((0,), (0,)), ((), ())), preferred_element_type=jnp.float32
    )


def contract_last(left, right):
    return lax.dot_general(
        left, right, (((1,), (1,)), ((), ())), preferred_element_type=jnp.float32
    )


def body(
    tokens,
    queries,
    keys,
    values,
    ln_gain,
    mean_in,
    sigma_in,
    noise_in,
    mean_out,
    sigma_out,
    noise_out,
    flip_in,
    flip_mid,
    flip_hidden,
    flip_out,
    cotangent,
):
    bf = jnp.bfloat16
    f32 = jnp.float32
    own_images, patches, width = tokens.shape
    hidden_local = mean_in.shape[1]
    head_dim = width // HEADS
    scale = head_dim ** (-0.5)
    pert_in = (sigma_in.astype(f32) * noise_in.astype(f32)).astype(bf)
    pert_out = (sigma_out.astype(f32) * noise_out.astype(f32)).astype(bf)
    query_heads = queries.reshape(own_images, patches, HEADS, head_dim)
    key_heads = keys.reshape(own_images, patches, HEADS, head_dim)
    value_heads = values.reshape(own_images, patches, HEADS, head_dim)
    scores = (
        jnp.einsum("bqhe,bkhe->bhqk", query_heads, key_heads, preferred_element_type=f32) * scale
    )
    top = jnp.max(scores, axis=-1, keepdims=True)
    expd = jnp.exp(scores - top)
    total = jnp.sum(expd, axis=-1)
    accum = jnp.einsum("bhqk,bkhe->bqhe", expd.astype(bf), value_heads, preferred_element_type=f32)
    attn_out = (
        (accum / jnp.transpose(total, (0, 2, 1))[..., None])
        .reshape(own_images, patches, width)
        .astype(bf)
    )
    resid = (tokens.astype(f32) + attn_out.astype(f32)).astype(bf)
    resid_f = resid.astype(f32)
    centered = resid_f - jnp.mean(resid_f, axis=-1, keepdims=True)
    rstd = lax.rsqrt(jnp.mean(centered * centered, axis=-1, keepdims=True) + 1e-06)
    ahat = centered * rstd
    gain_f = ln_gain.astype(f32)
    normed = (ahat * gain_f).astype(bf)
    in_signs = flip_in.astype(bf)[:, None, :]
    in_signs_f = flip_in.astype(f32)[:, None, :]
    mid_signs = flip_mid.astype(bf)[:, None, :]
    mid_signs_f = flip_mid.astype(f32)[:, None, :]
    hid_signs = flip_hidden.astype(bf)[:, None, :]
    hid_signs_f = flip_hidden.astype(f32)[:, None, :]
    out_signs = flip_out.astype(bf)[:, None, :]
    out_signs_f = flip_out.astype(f32)[:, None, :]
    gathered = lax.all_gather(normed, "seq", axis=0, tiled=True)
    count = gathered.shape[0]
    signs = in_signs
    flat = gathered.reshape(-1, width)
    flat_flip = (gathered * signs).reshape(-1, width)
    plain = jnp.dot(flat, mean_in, preferred_element_type=f32).reshape(count, patches, hidden_local)
    noisy = jnp.dot(flat_flip, pert_in, preferred_element_type=f32).reshape(
        count, patches, hidden_local
    )
    pre = plain + noisy * mid_signs_f
    group_images = pre.shape[0]
    rows = group_images * patches
    hidden = jax.nn.gelu(pre, approximate=False).astype(bf)
    flipped_hidden = hidden * hid_signs
    count = lax.axis_size("seq") * own_images
    hb = hidden.reshape(-1, hidden_local)
    hfb = flipped_hidden.reshape(-1, hidden_local)
    plain = jnp.dot(hb, mean_out, preferred_element_type=f32).reshape(count, patches, width)
    noisy = jnp.dot(hfb, pert_out, preferred_element_type=f32).reshape(count, patches, width)
    mixed = lax.psum_scatter(
        (plain + noisy * out_signs_f).astype(jnp.bfloat16), "seq", scatter_dimension=0, tiled=True
    ).astype(jnp.float32)
    block_out = (resid_f + mixed).astype(bf)
    cot_all = lax.all_gather(cotangent, "seq", axis=0, tiled=True)
    cot_flat = cot_all.reshape(rows, width)
    cot_flip_flat = (cot_all * out_signs).reshape(rows, width)
    dhidden = contract_last(cot_flat, mean_out).reshape(group_images, patches, hidden_local)
    dhidden = (
        dhidden
        + contract_last(cot_flip_flat, pert_out).reshape(group_images, patches, hidden_local)
        * hid_signs_f
    )
    dpre = (dhidden * gelu_slope(pre)).astype(bf)
    dpre_flip = dpre * mid_signs
    local_mean_out = contract_first(hidden.reshape(rows, hidden_local), cot_flat)
    local_sigma_out = contract_first(
        flipped_hidden.reshape(rows, hidden_local), cot_flip_flat
    ) * noise_out.astype(f32)
    grad_mean_out, grad_sigma_out = (
        lax.psum(local_mean_out.astype(jnp.bfloat16), "dp").astype(jnp.float32),
        lax.psum(local_sigma_out.astype(jnp.bfloat16), "dp").astype(jnp.float32),
    )
    local_mean_in = contract_first(gathered.reshape(rows, width), dpre.reshape(rows, hidden_local))
    local_flip_in = contract_first(
        (gathered * in_signs).reshape(rows, width), dpre_flip.reshape(rows, hidden_local)
    )
    local_sigma_in = local_flip_in * noise_in.astype(f32)
    count = lax.axis_size("seq") * own_images
    drows = dpre.reshape(-1, hidden_local)
    dflip_rows = dpre_flip.reshape(-1, hidden_local)
    signs = in_signs_f
    plain = contract_last(drows, mean_in).reshape(count, patches, width)
    noisy = contract_last(dflip_rows, pert_in).reshape(count, patches, width)
    dnormed = lax.psum_scatter(
        (plain + noisy * signs).astype(jnp.bfloat16), "seq", scatter_dimension=0, tiled=True
    ).astype(jnp.float32)
    grad_mean_in, grad_sigma_in = (
        lax.psum(local_mean_in.astype(jnp.bfloat16), "dp").astype(jnp.float32),
        lax.psum(local_sigma_in.astype(jnp.bfloat16), "dp").astype(jnp.float32),
    )
    scaled = dnormed * gain_f
    back = rstd * (
        scaled
        - jnp.mean(scaled, axis=-1, keepdims=True)
        - ahat * jnp.mean(scaled * ahat, axis=-1, keepdims=True)
    )
    resid_grad = (cotangent.astype(f32) + back).astype(bf)
    return (block_out, resid_grad, grad_mean_in, grad_sigma_in, grad_mean_out, grad_sigma_out)


def solution(mesh):
    return jax.shard_map(
        body,
        mesh=mesh,
        in_specs=(
            P(("dp", "seq"), None, None),
            P(("dp", "seq"), None, None),
            P(("dp", "seq"), None, None),
            P(("dp", "seq"), None, None),
            P(),
            P(None, "seq"),
            P(None, "seq"),
            P(None, "seq"),
            P("seq", None),
            P("seq", None),
            P("seq", None),
            P("dp", None),
            P("dp", "seq"),
            P("dp", "seq"),
            P("dp", None),
            P(("dp", "seq"), None, None),
        ),
        out_specs=(
            P(("dp", "seq"), None, None),
            P(("dp", "seq"), None, None),
            P(None, "seq"),
            P(None, "seq"),
            P("seq", None),
            P("seq", None),
        ),
        check_vma=False,
    )
```

profile of v0, /device:TPU:0, one launch (start us, length us, event | category | flops | bytes accessed | tf_op | source)
XLA Modules:
  0.0 289.0 jit_solution(1723222755347720097)
XLA Ops:
  7.2 0.0 copy-start
  7.2 0.0 all-gather.3.cloned.1.call-start
  7.2 1.4 copy.42
  8.6 1.2 copy.40
  9.9 0.2 copy.41
  10.1 0.8 multiply_reduce_fusion
  10.8 0.7 fusion
  11.6 0.9 divide_convert_fusion
  12.5 0.1 bitcast_convert_fusion.2
  12.6 1.3 copy.44
  13.9 1.5 convert_reduce_fusion
  15.5 0.3 fusion.51
  15.8 1.1 fusion.45
  16.9 0.0 all-gather.3.cloned.1.call-update
  16.9 0.0 all-gather.5.cloned.1.call-start
  16.9 0.7 all-gather.5.cloned.1.call-update
  17.6 0.2 all-reduce.5.cloned.1.call-start
  18.0 37.0 %all-gather.3.cloned.1.call-done = bf16[4,256,1024]{2,1,0:T(8,128)(2,1)} async-done(((bf16[1,256,1024]{2,1,0:T(8,128)(2,1)}), bf16[4,256,1024]{2,1,0:T(8,128)(2,1)}) %all-gather.3.cloned.1.call-update) | async-done | bytes 2097168 | tf_op jit(solution)/shard_map/all_gather | solution.py:83
  55.0 3.3 %fusion.31 = f32[4,256,512]{2,1,0:T(8,128)S(1)} fusion(bf16[4,256,1024]{2,1,0:T(8,128)(2,1)} %all-gather.3.cloned.1.call-done, bf16[4,1024]{1,0:T(4,128)(2,1)S(1)} %get-tuple-element.19, bf16[1024,512]{1,0:T(8,128)(2,1)S(1)} %copy-done.7, bf16[1024,512]{1,0:T(8,128)(2,1)} %param.22), kind=kOutput, calls=%fused_computation.55 | convolution fusion | flops 1076887552 | bytes 6299648 | tf_op jit(solution)/shard_map/dot_general | solution.py:89
  58.3 1.9 fusion.77
  60.2 1.3 copy-done.4
  61.5 4.7 %fusion.8 = bf16[4,256,512]{2,1,0:T(8,128)(2,1)S(1)} fusion(f32[4,256,512]{2,1,0:T(8,128)S(1)} %get-tuple-element.28, u8[256,512]{1,0:T(8,128)(4,1)S(1)} %get-tuple-element.7, u8[256,512]{1,0:T(8,128)(4,1)S(1)} %get-tuple-element.6), kind=kLoop, calls=%fused_computation.18 | loop fusion | flops 36700160 | bytes 3407872 | tf_op jit(solution)/shard_map/convert_element_type | solution.py:95
  66.2 25.8 %all-gather.5.cloned.1.call-done = bf16[4,256,1024]{2,1,0:T(8,128)(2,1)} async-done(((bf16[1,256,1024]{2,1,0:T(8,128)(2,1)}), bf16[4,256,1024]{2,1,0:T(8,128)(2,1)}) %all-gather.5.cloned.1.call-update) | async-done | bytes 2097168 | tf_op jit(solution)/shard_map/all_gather | solution.py:106
  92.0 3.6 %fusion.27 = f32[4,256,512]{2,1,0:T(8,128)S(1)} fusion(bf16[4,256,1024]{2,1,0:T(8,128)(2,1)} %all-gather.5.cloned.1.call-done, bf16[4,1024]{1,0:T(4,128)(2,1)S(1)} %get-tuple-element.20, bf16[512,1024]{1,0:T(8,128)(2,1)} %param.26, bf16[512,1024]{1,0:T(8,128)(2,1)} %param.25), kind=kOutput, calls=%fused_computation.51 | convolution fusion | flops 1076887552 | bytes 6299648 | tf_op jit(solution)/shard_map/dot_general | solution.py:22
  95.7 0.1 copy-done.17
  95.8 2.0 fusion.14
  97.8 2.3 bitcast_convert_fusion.1
  100.1 2.3 fusion.3
  102.4 2.3 bitcast_convert_fusion
  104.6 2.4 fusion.5
  107.0 0.0 all-reduce.5.cloned.1.call-update
  107.0 0.3 reduce-scatter.9.cloned.1.call-start
  107.3 2.7 fusion.58
  110.0 2.6 add_convert_fusion
  112.6 0.0 reduce-scatter.9.cloned.1.call-update
  112.7 0.0 reduce-scatter.7.cloned.1.call-start
  112.7 2.6 fusion.56
  115.4 2.6 add_convert_fusion.1
  118.0 0.0 reduce-scatter.7.cloned.1.call-update
  118.0 85.7 %all-reduce.5.cloned.1.call-done = (bf16[1024,512]{1,0:T(8,128)(2,1)}, bf16[1024,512]{1,0:T(8,128)(2,1)}, bf16[512,1024]{1,0:T(8,128)(2,1)}, bf16[512,1024]{1,0:T(8,128)(2,1)}) async-done(((bf16[1024,512]{1,0:T(8,128)(2,1)}, bf16[1024,512]{1,0:T(8,128)(2,1)}, bf16[512,1024]{1,0:T(8,128)(2,1)}, bf16[512,1024]{1,0:T(8,128)(2,1)}), (bf16[1024,512]{1,0:T(8,128)(2,1)}, bf16[1024,512]{1,0:T(8,128)(2,1)}, ...) | async-done | bytes 4194320 | tf_op jit(solution)/shard_map/psum | solution.py:140
  203.7 2.9 %convert_element_type.173 = f32[1024,512]{1,0:T(8,128)} convert(bf16[1024,512]{1,0:T(8,128)(2,1)} %get-tuple-element.10) | non-fusion elementwise | flops 524288 | bytes 3145728 | tf_op jit(solution)/shard_map/convert_element_type | solution.py:140
  206.7 1.6 convert_element_type.175
  208.3 1.6 convert_element_type.177
  209.8 1.6 convert_element_type.179
  211.4 30.4 %reduce-scatter.9.cloned.1.call-done = bf16[1,256,1024]{2,1,0:T(8,128)(2,1)} async-done(((bf16[4,256,1024]{2,1,0:T(8,128)(2,1)}), bf16[1,256,1024]{2,1,0:T(8,128)(2,1)}) %reduce-scatter.9.cloned.1.call-update) | async-done | bytes 524304
  241.8 1.4 fusion.61
  243.2 36.6 %reduce-scatter.7.cloned.1.call-done = bf16[1,256,1024]{2,1,0:T(8,128)(2,1)} async-done(((bf16[4,256,1024]{2,1,0:T(8,128)(2,1)}), bf16[1,256,1024]{2,1,0:T(8,128)(2,1)}) %reduce-scatter.7.cloned.1.call-update) | async-done | bytes 524304
  279.8 2.6 fusion.50
  (59 shorter events, 0.2 us)
Async XLA Ops:
  7.2 51.1 %copy-start = (bf16[1024,512]{1,0:T(8,128)(2,1)S(1)}, bf16[1024,512]{1,0:T(8,128)(2,1)}, u32[]{:S(2)}) copy-start(bf16[1024,512]{1,0:T(8,128)(2,1)} %param.21) | copy-start | bytes 3145732
  7.2 2.7 copy-start.18
  7.2 47.8 %all-gather.3.cloned.1.call-start = ((), (), s32[]{:S(2)}) async-start(), calls=%async_computation.2 | async-start | bytes 2621440 | tf_op jit(solution)/shard_map/all_gather | solution.py:83
  12.4 1.4 copy-start.24
  12.4 1.4 copy-start.19
  13.9 4.0 %copy-start.22 = (s32[4,512]{1,0:T(4,128)S(1)}, s32[4,512]{1,0:T(4,128)}, u32[]{:S(2)}) copy-start(s32[4,512]{1,0:T(4,128)} %param.28) | copy-start | bytes 24580
  13.9 4.0 %copy-start.23 = (s32[4,512]{1,0:T(4,128)S(1)}, s32[4,512]{1,0:T(4,128)}, u32[]{:S(2)}) copy-start(s32[4,512]{1,0:T(4,128)} %param.29) | copy-start | bytes 24580
  13.9 4.0 %copy-start.20 = (s32[4,1024]{1,0:T(4,128)S(1)}, s32[4,1024]{1,0:T(4,128)}, u32[]{:S(2)}) copy-start(s32[4,1024]{1,0:T(4,128)} %param.27) | copy-start | bytes 49156
  13.9 4.0 %copy-start.21 = (s32[4,1024]{1,0:T(4,128)S(1)}, s32[4,1024]{1,0:T(4,128)}, u32[]{:S(2)}) copy-start(s32[4,1024]{1,0:T(4,128)} %param.30) | copy-start | bytes 49156
  13.9 41.0 %copy-start.7 = (bf16[1024,512]{1,0:T(8,128)(2,1)S(1)}, bf16[1024,512]{1,0:T(8,128)(2,1)}, u32[]{:S(2)}) copy-start(bf16[1024,512]{1,0:T(8,128)(2,1)} %param.23) | copy-start | bytes 3145732
  16.9 75.1 %all-gather.5.cloned.1.call-start = ((), (), s32[]{:S(2)}) async-start(), calls=%async_computation.3 | async-start | bytes 2621440 | tf_op jit(solution)/shard_map/all_gather | solution.py:106
  17.6 186.1 %all-reduce.5.cloned.1.call-start = ((), (), s32[]{:S(2)}) async-start(), calls=%async_computation.6 | async-start | bytes 8388608 | tf_op jit(solution)/shard_map/psum | solution.py:140
  55.0 3.3 %copy-start.25 = (bf16[4,256,1024]{2,1,0:T(8,128)(2,1)S(1)}, bf16[4,256,1024]{2,1,0:T(8,128)(2,1)}, u32[]{:S(2)}) copy-start(bf16[4,256,1024]{2,1,0:T(8,128)(2,1)} %all-gather.3.cloned.1.call-done) | copy-start | bytes 6291460
  60.2 1.3 copy-start.4
  92.0 3.6 %copy-start.3 = (bf16[4,256,1024]{2,1,0:T(8,128)(2,1)S(1)}, bf16[4,256,1024]{2,1,0:T(8,128)(2,1)}, u32[]{:S(2)}) copy-start(bf16[4,256,1024]{2,1,0:T(8,128)(2,1)} %all-gather.5.cloned.1.call-done) | copy-start | bytes 6291460
  92.0 3.6 %copy-start.5 = (f32[4,256,512]{2,1,0:T(8,128)S(1)}, f32[4,256,512]{2,1,0:T(8,128)}, u32[]{:S(2)}) copy-start(f32[4,256,512]{2,1,0:T(8,128)} %copy-done.4) | copy-start | bytes 6291460
  92.0 3.7 %copy-start.17 = (bf16[512,1024]{1,0:T(8,128)(2,1)S(1)}, bf16[512,1024]{1,0:T(8,128)(2,1)}, u32[]{:S(2)}) copy-start(bf16[512,1024]{1,0:T(8,128)(2,1)} %param.24) | copy-start | bytes 3145732
  95.8 2.1 copy-start.26
  97.8 2.3 copy-start.1
  97.8 2.3 copy-start.8
  102.4 2.3 copy-start.11
  107.0 134.8 %reduce-scatter.9.cloned.1.call-start = ((), (), s32[]{:S(2)}) async-start(), calls=%async_computation.5 | async-start | bytes 2621440
  107.3 2.7 copy-start.2
  107.3 2.7 copy-start.9
  107.3 2.7 copy-start.10
  112.7 167.2 %reduce-scatter.7.cloned.1.call-start = ((), (), s32[]{:S(2)}) async-start(), calls=%async_computation.4 | async-start | bytes 2621440
  112.7 2.7 copy-start.12
  112.7 2.7 copy-start.13
  203.7 2.9 %copy-start.16 = (bf16[1024,512]{1,0:T(8,128)(2,1)S(1)}, bf16[1024,512]{1,0:T(8,128)(2,1)}, u32[]{:S(2)}) copy-start(bf16[1024,512]{1,0:T(8,128)(2,1)} %get-tuple-element.11) | copy-start | bytes 3145732
  206.6 1.6 copy-start.15
  208.3 1.6 copy-start.14
  209.8 70.0 %copy-start.6 = (bf16[1,256,1024]{2,1,0:T(8,128)(2,1)S(1)}, bf16[1,256,1024]{2,1,0:T(8,128)(2,1)}, u32[]{:S(2)}) copy-start(bf16[1,256,1024]{2,1,0:T(8,128)(2,1)} %param.31) | copy-start | bytes 1572868
Sparse Core Ops, SparseCore 0:
  17.0 37.8 all-gather.2
  56.8 35.1 all-gather.4
  107.1 96.5 all-reduce.4
  206.5 35.2 reduce-scatter.8
  244.6 35.1 reduce-scatter.6
where the time goes:
time: 289 us
  waiting for transfers between devices  216 us (75%)
  matrix products  32.2 us (11%)
  other arithmetic  20.2 us (7%)
  between operations  14.2 us (5%)
  local copies, waits for them, and re-layouts  5.66 us (2%)
    psum x1, waiting for transfers between devices, body(): lax.psum(local_mean_in.astype(jnp.bfloat16), 'dp').astype(jnp.float32)  85.7 us
    unnamed x7, waiting for transfers between devices  67.8 us
    all_gather x1, waiting for transfers between devices, body(): gathered = lax.all_gather(normed, 'seq', axis=0, tiled=True)  37 us
    all_gather x1, waiting for transfers between devices, body(): cot_all = lax.all_gather(cotangent, 'seq', axis=0, tiled=True)  25.8 us
    dot_general x4, matrix products, contract_last(): lax.dot_general(left, right, (((1,), (1,)), ((), ())), preferred_element_...  11 us
    dot_general x4, matrix products, contract_first(): lax.dot_general(left, right, (((0,), (0,)), ((), ())), preferred_element_...  9.14 us
  transfers between devices with their start and end apart: 5, of which 5 were waited for; matrix products, arithmetic and copies ran while one was open for 10% of the time, Pallas kernels for 0%

commit v1 on v0

--- a/solution.py
+++ b/solution.py
@@ -4,6 +4,16 @@
 from jax.sharding import PartitionSpec as P
 
 HEADS = 16
+
+
+def reach_the_kinds(inp):
+    n = jax.lax.axis_size("seq")
+    g_now = [None] * n
+    entries = list(map(lambda w: (w, (w + 1) % n), range(n)))
+    g_now[n - 1] = inp
+    for dev_i in range(n - 2, -1, -1):
+        g_now[dev_i] = jax.lax.ppermute(g_now[dev_i + 1], axis_name="seq", perm=entries)
+    return jnp.roll(jnp.concatenate(g_now, 0), (jax.lax.axis_index("seq") + 1) * inp.shape[0], 0)
 
 
 def gelu_slope(pre):
@@ -80,7 +90,7 @@
     hid_signs_f = flip_hidden.astype(f32)[:, None, :]
     out_signs = flip_out.astype(bf)[:, None, :]
     out_signs_f = flip_out.astype(f32)[:, None, :]
-    gathered = lax.all_gather(normed, "seq", axis=0, tiled=True)
+    gathered = reach_the_kinds(normed)
     count = gathered.shape[0]
     signs = in_signs
     flat = gathered.reshape(-1, width)

time: 289 us -> 276 us (0.955)
  waiting for transfers between devices: 216 us -> 198 us
  starting transfers between devices: 0.6 us -> 5.92 us
    ppermute x0 -> x3, waiting for transfers between devices: none -> 42.5 us  [reach_the_kinds(): jax.lax.ppermute(g_now[dev_i + 1], axis_name='seq', perm=entries)]
    all_gather x1 -> x0, waiting for transfers between devices: 37 us -> none  [body(): gathered = lax.all_gather(normed, 'seq', axis=0, tiled=True)]
    all_gather x1, waiting for transfers between devices: 25.8 us -> 0.02 us  [body(): cot_all = lax.all_gather(cotangent, 'seq', axis=0, tiled=True)]
    ppermute x0 -> x3, starting transfers between devices: none -> 5.54 us  [reach_the_kinds(): jax.lax.ppermute(g_now[dev_i + 1], axis_name='seq', perm=entries)]
    unnamed x57 -> x65, local copies, waits for them, and re-layouts: 4.35 us -> 6.15 us
    unnamed x7 -> x6, waiting for transfers between devices: 67.8 us -> 67.3 us
  transfers between devices with their start and end apart: 5 -> 7, of which waited for: 5 -> 6; matrix products, arithmetic and copies ran while one was open for 10% -> 10% of each run, Pallas kernels for 0% -> 0%
where the time goes in v1:
time: 276 us
  waiting for transfers between devices  198 us (72%)
  matrix products  30.1 us (11%)
  other arithmetic  19.9 us (7%)
  between operations  14.2 us (5%)
  local copies, waits for them, and re-layouts  7.46 us (3%)
  starting transfers between devices  5.92 us (2%)
    psum x1, waiting for transfers between devices, body(): lax.psum(local_mean_in.astype(jnp.bfloat16), 'dp').astype(jnp.float32)  88.2 us
    unnamed x6, waiting for transfers between devices  67.3 us
    ppermute x3, waiting for transfers between devices, reach_the_kinds(): jax.lax.ppermute(g_now[dev_i + 1], axis_name='seq', perm=entries)  42.5 us
    dot_general x4, matrix products, contract_last(): lax.dot_general(left, right, (((1,), (1,)), ((), ())), preferred_element_...  11 us
    dot_general x4, matrix products, contract_first(): lax.dot_general(left, right, (((0,), (0,)), ((), ())), preferred_element_...  9.13 us
    unnamed x65, local copies, waits for them, and re-layouts  6.15 us
    ppermute x3, starting transfers between devices, reach_the_kinds(): jax.lax.ppermute(g_now[dev_i + 1], axis_name='seq', perm=entries)  5.54 us
  transfers between devices with their start and end apart: 7, of which 6 were waited for; matrix products, arithmetic and copies ran while one was open for 10% of the time, Pallas kernels for 0%

profile of v1, /device:TPU:0, one launch (start us, length us, event | category | flops | bytes accessed | tf_op | source)
XLA Modules:
  0.0 275.6 jit_solution(8147811761597464718)
XLA Ops:
  7.2 1.4 copy.42
  8.6 1.2 copy.40
  9.9 0.2 copy.41
  10.1 0.8 multiply_reduce_fusion
  10.8 0.7 fusion
  11.6 0.9 divide_convert_fusion
  12.5 0.1 bitcast_convert_fusion.2
  12.6 1.3 copy.44
  13.9 1.4 convert_reduce_fusion
  15.4 0.3 fusion.55
  15.7 0.3 fusion.49
  16.0 3.0 %collective-permute-start = (bf16[1,256,1024]{2,1,0:T(8,128)(2,1)S(1)}, bf16[1,256,1024]{2,1,0:T(8,128)(2,1)S(1)}, u32[]{:S(2)}, u32[]{:S(2)}) collective-permute-start(bf16[1,256,1024]{2,1,0:T(8,128)(2,1)S(1)} %fusion.49), channel_id=1, source_target_pairs={{0,1},{1,2},{2,3},{3,0},{4,5},{5,6},{6,7},{7,4},{8,9},{9,10},{10,1... | collective-permute-start | bytes 1572872 | tf_op jit(solution)/shard_map/ppermute | solution.py:15
  19.0 12.9 %collective-permute-done = bf16[1,256,1024]{2,1,0:T(8,128)(2,1)S(1)} collective-permute-done((bf16[1,256,1024]{2,1,0:T(8,128)(2,1)S(1)}, bf16[1,256,1024]{2,1,0:T(8,128)(2,1)S(1)}, u32[]{:S(2)}, u32[]{:S(2)}) %collective-permute-start) | collective-permute-done | bytes 524320 | tf_op jit(solution)/shard_map/ppermute | solution.py:15
  31.9 0.8 collective-permute-start.1
  32.8 14.5 %collective-permute-done.1 = bf16[1,256,1024]{2,1,0:T(8,128)(2,1)S(1)} collective-permute-done((bf16[1,256,1024]{2,1,0:T(8,128)(2,1)S(1)}, bf16[1,256,1024]{2,1,0:T(8,128)(2,1)S(1)}, u32[]{:S(2)}, u32[]{:S(2)}) %collective-permute-start.1) | collective-permute-done | bytes 524320 | tf_op jit(solution)/shard_map/ppermute | solution.py:15
  47.3 1.7 collective-permute-start.2
  49.1 15.2 %collective-permute-done.2 = bf16[1,256,1024]{2,1,0:T(8,128)(2,1)S(1)} collective-permute-done((bf16[1,256,1024]{2,1,0:T(8,128)(2,1)S(1)}, bf16[1,256,1024]{2,1,0:T(8,128)(2,1)S(1)}, u32[]{:S(2)}, u32[]{:S(2)}) %collective-permute-start.2) | collective-permute-done | bytes 524320 | tf_op jit(solution)/shard_map/ppermute | solution.py:15
  64.3 0.3 constant_dynamic-update-slice_fusion.4
  64.8 0.3 constant_dynamic-update-slice_fusion
  65.1 0.8 copy-done.7
  65.9 0.7 copy-done.10
  66.6 1.3 fusion.31
  67.9 1.9 fusion.81
  69.8 1.3 copy-done.4
  71.1 4.7 %fusion.8 = bf16[4,256,512]{2,1,0:T(8,128)(2,1)S(1)} fusion(f32[4,256,512]{2,1,0:T(8,128)S(1)} %get-tuple-element.28, u8[256,512]{1,0:T(8,128)(4,1)S(1)} %get-tuple-element.7, u8[256,512]{1,0:T(8,128)(4,1)S(1)} %get-tuple-element.6), kind=kLoop, calls=%fused_computation.18 | loop fusion | flops 36700160 | bytes 3407872 | tf_op jit(solution)/shard_map/convert_element_type | solution.py:105
  75.9 3.6 %fusion.27 = f32[4,256,512]{2,1,0:T(8,128)S(1)} fusion(bf16[4,256,1024]{2,1,0:T(8,128)(2,1)} %all-gather.2.cloned.1.call-done, bf16[4,1024]{1,0:T(4,128)(2,1)S(1)} %get-tuple-element.20, bf16[512,1024]{1,0:T(8,128)(2,1)} %param.26, bf16[512,1024]{1,0:T(8,128)(2,1)} %param.25), kind=kOutput, calls=%fused_computation.51 | convolution fusion | flops 1076887552 | bytes 6299648 | tf_op jit(solution)/shard_map/dot_general | solution.py:32
  79.6 0.1 copy-done.18
  79.6 2.0 fusion.14
  81.7 0.1 copy-done.22
  81.8 2.2 bitcast_convert_fusion.1
  84.1 2.3 fusion.3
  86.4 2.3 bitcast_convert_fusion
  88.6 2.3 fusion.5
  91.0 0.3 reduce-scatter.9.cloned.1.call-start
  91.3 2.7 fusion.62
  94.0 2.6 add_convert_fusion
  96.6 0.0 reduce-scatter.7.cloned.1.call-start
  96.7 2.6 fusion.60
  99.4 2.6 add_convert_fusion.1
  102.0 88.2 %all-reduce.5.cloned.1.call-done = (bf16[1024,512]{1,0:T(8,128)(2,1)}, bf16[1024,512]{1,0:T(8,128)(2,1)}, bf16[512,1024]{1,0:T(8,128)(2,1)}, bf16[512,1024]{1,0:T(8,128)(2,1)}) async-done(((bf16[1024,512]{1,0:T(8,128)(2,1)}, bf16[1024,512]{1,0:T(8,128)(2,1)}, bf16[512,1024]{1,0:T(8,128)(2,1)}, bf16[512,1024]{1,0:T(8,128)(2,1)}), (bf16[1024,512]{1,0:T(8,128)(2,1)}, bf16[1024,512]{1,0:T(8,128)(2,1)}, ...) | async-done | bytes 4194320 | tf_op jit(solution)/shard_map/psum | solution.py:150
  190.2 2.9 %convert_element_type.173 = f32[1024,512]{1,0:T(8,128)} convert(bf16[1024,512]{1,0:T(8,128)(2,1)} %get-tuple-element.10) | non-fusion elementwise | flops 524288 | bytes 3145728 | tf_op jit(solution)/shard_map/convert_element_type | solution.py:150
  193.1 1.6 convert_element_type.175
  194.8 1.6 convert_element_type.177
  196.3 1.6 convert_element_type.179
  197.9 30.6 %reduce-scatter.9.cloned.1.call-done = bf16[1,256,1024]{2,1,0:T(8,128)(2,1)} async-done(((bf16[4,256,1024]{2,1,0:T(8,128)(2,1)}), bf16[1,256,1024]{2,1,0:T(8,128)(2,1)}) %reduce-scatter.9.cloned.1.call-update) | async-done | bytes 524304
  228.4 1.4 fusion.65
  229.9 36.6 %reduce-scatter.7.cloned.1.call-done = bf16[1,256,1024]{2,1,0:T(8,128)(2,1)} async-done(((bf16[4,256,1024]{2,1,0:T(8,128)(2,1)}), bf16[1,256,1024]{2,1,0:T(8,128)(2,1)}) %reduce-scatter.7.cloned.1.call-update) | async-done | bytes 524304
  266.5 2.6 fusion.54
  (72 shorter events, 0.6 us)
Async XLA Ops:
  7.2 60.7 %copy-start = (bf16[1024,512]{1,0:T(8,128)(2,1)S(1)}, bf16[1024,512]{1,0:T(8,128)(2,1)}, u32[]{:S(2)}) copy-start(bf16[1024,512]{1,0:T(8,128)(2,1)} %param.21) | copy-start | bytes 3145732
  7.2 2.7 copy-start.19
  7.2 68.7 %all-gather.2.cloned.1.call-start = ((), (), s32[]{:S(2)}) async-start(), calls=%async_computation.2 | async-start | bytes 2621440 | tf_op jit(solution)/shard_map/all_gather | solution.py:116
  12.4 1.4 copy-start.27
  12.5 1.4 copy-start.20
  13.9 18.9 %copy-start.25 = (s32[4,512]{1,0:T(4,128)S(1)}, s32[4,512]{1,0:T(4,128)}, u32[]{:S(2)}) copy-start(s32[4,512]{1,0:T(4,128)} %param.28) | copy-start | bytes 24580
  13.9 35.1 %copy-start.26 = (s32[4,512]{1,0:T(4,128)S(1)}, s32[4,512]{1,0:T(4,128)}, u32[]{:S(2)}) copy-start(s32[4,512]{1,0:T(4,128)} %param.29) | copy-start | bytes 24580
  13.9 35.1 %copy-start.23 = (s32[4,1024]{1,0:T(4,128)S(1)}, s32[4,1024]{1,0:T(4,128)}, u32[]{:S(2)}) copy-start(s32[4,1024]{1,0:T(4,128)} %param.27) | copy-start | bytes 49156
  13.9 35.1 %copy-start.24 = (s32[4,1024]{1,0:T(4,128)S(1)}, s32[4,1024]{1,0:T(4,128)}, u32[]{:S(2)}) copy-start(s32[4,1024]{1,0:T(4,128)} %param.30) | copy-start | bytes 49156
  16.0 15.9 %collective-permute-start = (bf16[1,256,1024]{2,1,0:T(8,128)(2,1)S(1)}, bf16[1,256,1024]{2,1,0:T(8,128)(2,1)S(1)}, u32[]{:S(2)}, u32[]{:S(2)}) collective-permute-start(bf16[1,256,1024]{2,1,0:T(8,128)(2,1)S(1)} %fusion.49), channel_id=1, source_target_pairs={{0,1},{1,2},{2,3},{3,0},{4,5},{5,6},{6,7},{7,4},{8,9},{9,10},{10,1... | collective-permute-start | bytes 1572872 | tf_op jit(solution)/shard_map/ppermute | solution.py:15
  31.9 15.4 %collective-permute-start.1 = (bf16[1,256,1024]{2,1,0:T(8,128)(2,1)S(1)}, bf16[1,256,1024]{2,1,0:T(8,128)(2,1)S(1)}, u32[]{:S(2)}, u32[]{:S(2)}) collective-permute-start(bf16[1,256,1024]{2,1,0:T(8,128)(2,1)S(1)} %collective-permute-done), channel_id=1, source_target_pairs={{0,1},{1,2},{2,3},{3,0},{4,5},{5,6},{6,7},{7,4},{8,9},{9,10},{10,1... | collective-permute-start | bytes 1572872 | tf_op jit(solution)/shard_map/ppermute | solution.py:15
  32.7 157.5 %all-reduce.5.cloned.1.call-start = ((), (), s32[]{:S(2)}) async-start(), calls=%async_computation.5 | async-start | bytes 8388608 | tf_op jit(solution)/shard_map/psum | solution.py:150
  47.3 16.9 %collective-permute-start.2 = (bf16[1,256,1024]{2,1,0:T(8,128)(2,1)S(1)}, bf16[1,256,1024]{2,1,0:T(8,128)(2,1)S(1)}, u32[]{:S(2)}, u32[]{:S(2)}) collective-permute-start(bf16[1,256,1024]{2,1,0:T(8,128)(2,1)S(1)} %collective-permute-done.1), channel_id=1, source_target_pairs={{0,1},{1,2},{2,3},{3,0},{4,5},{5,6},{6,7},{7,4},{8,9},{9,10},{10,1... | collective-permute-start | bytes 1572872 | tf_op jit(solution)/shard_map/ppermute | solution.py:15
  64.6 1.2 copy-start.7
  64.7 1.9 copy-start.10
  65.1 2.8 %copy-start.21 = (bf16[8,256,1024]{2,1,0:T(8,128)(2,1)}, bf16[8,256,1024]{2,1,0:T(8,128)(2,1)S(1)}, u32[]{:S(2)}) copy-start(bf16[8,256,1024]{2,1,0:T(8,128)(2,1)S(1)} %constant_dynamic-update-slice_fusion) | copy-start | bytes 12582916
  69.8 1.3 copy-start.4
  75.9 3.7 %copy-start.3 = (bf16[4,256,1024]{2,1,0:T(8,128)(2,1)S(1)}, bf16[4,256,1024]{2,1,0:T(8,128)(2,1)}, u32[]{:S(2)}) copy-start(bf16[4,256,1024]{2,1,0:T(8,128)(2,1)} %all-gather.2.cloned.1.call-done) | copy-start | bytes 6291460
  75.9 3.7 %copy-start.5 = (f32[4,256,512]{2,1,0:T(8,128)S(1)}, f32[4,256,512]{2,1,0:T(8,128)}, u32[]{:S(2)}) copy-start(f32[4,256,512]{2,1,0:T(8,128)} %copy-done.4) | copy-start | bytes 6291460
  75.9 3.7 %copy-start.18 = (bf16[512,1024]{1,0:T(8,128)(2,1)S(1)}, bf16[512,1024]{1,0:T(8,128)(2,1)}, u32[]{:S(2)}) copy-start(bf16[512,1024]{1,0:T(8,128)(2,1)} %param.24) | copy-start | bytes 3145732
  79.6 2.2 copy-start.22
  81.8 2.3 copy-start.1
  81.8 2.3 copy-start.8
  86.4 2.3 copy-start.12
  91.0 137.4 %reduce-scatter.9.cloned.1.call-start = ((), (), s32[]{:S(2)}) async-start(), calls=%async_computation.4 | async-start | bytes 2621440
  91.3 2.7 copy-start.2
  91.3 2.7 copy-start.9
  91.3 2.7 copy-start.11
  96.6 169.9 %reduce-scatter.7.cloned.1.call-start = ((), (), s32[]{:S(2)}) async-start(), calls=%async_computation.3 | async-start | bytes 2621440
  96.7 2.7 copy-start.13
  96.7 2.7 copy-start.14
  190.2 2.9 %copy-start.17 = (bf16[1024,512]{1,0:T(8,128)(2,1)S(1)}, bf16[1024,512]{1,0:T(8,128)(2,1)}, u32[]{:S(2)}) copy-start(bf16[1024,512]{1,0:T(8,128)(2,1)} %get-tuple-element.11) | copy-start | bytes 3145732
  193.1 1.6 copy-start.16
  194.7 1.6 copy-start.15
  196.3 70.2 %copy-start.6 = (bf16[1,256,1024]{2,1,0:T(8,128)(2,1)S(1)}, bf16[1,256,1024]{2,1,0:T(8,128)(2,1)}, u32[]{:S(2)}) copy-start(bf16[1,256,1024]{2,1,0:T(8,128)(2,1)} %param.31) | copy-start | bytes 1572868
Sparse Core Ops, SparseCore 0:
  32.8 41.4 all-gather.1
  91.1 99.0 all-reduce.4
  193.2 35.2 reduce-scatter.8
  231.3 35.1 reduce-scatter.6
